TPU v7x, 32 devices: a whole 2x2x4 slice. The times are simulated.
32 devices in a mesh: seq: 8 (over z, y), mp: 4 (over x, core).
Axes of the slice: x: 2, y: 2, z: 4, core: 2. Of those that a mesh axis runs over, the one named last changes fastest.
Arguments:
- resid: bfloat16 [2048, 5120], P('seq', 'mp'), may hold values from -15 to 15
- queries: bfloat16 [2048, 5120], P('seq', 'mp'), may hold values from -28 to 28
- keys: bfloat16 [2048, 5120], P('seq', 'mp'), may hold values from -12.25 to 12.25
- values: bfloat16 [2048, 5120], P('seq', 'mp'), may hold values from -6 to 6
- doc_ids: int32 [2048], P('seq'), may hold values from 0 to 3, as said below
- out_proj: bfloat16 [5120, 5120], P('mp'), may hold values from -0.5 to 0.5
- ffn_gain: bfloat16 [5120], P('mp'), may hold values from 0.25 to 1.75
- w_in: bfloat16 [5120, 13824], P('mp', 'seq'), may hold values from -0.078125 to 0.078125
- w_out: bfloat16 [13824, 5120], P('seq', 'mp'), may hold values from -0.109375 to 0.109375
- hot_index: int32 [8, 384], P('seq'), may hold values from 0 to 1727, as said below
- hot_blocks: int32 [8], P('seq'), may hold values from 1 to 3, as said below
Outputs:
- layer_out: bfloat16 [2048, 5120], P('seq', 'mp')
- hot_mean: float32 [8, 384], P('seq')
Inputs may be any that keep to these rules, and one draw needn't show every extreme that they name: `doc_ids`: document numbers never fall along the tokens; every number from 0 to 3 occurs; some document has 1024 tokens. `hot_index`: row g holds 384 distinct neuron numbers of group g; only its first 128 * hot_blocks[g] entries are live, the others are ignored. `hot_blocks`: some group has exactly 3 live blocks.
All inputs are finite; a program needn't handle non-finite values.
Results may differ from a plain program's by a relative error of at most 0.014.
Values may be sent and summed in bfloat16 or wider, within the bound.
A program may use at most 192 MiB of HBM per device.

v0:
```python
import jax
import jax.numpy as jnp
from jax import lax
from jax.sharding import PartitionSpec as P

D = 5120
HEAD_DIM = 128
BLOCK = 128


epsilon = 1e-05
masked_score = -1e30


def attend_block(
    state, query_rows, query_pos, query_docs, key_rows, value_rows, key_pos, key_docs, scale
):
    top, total, accum = state
    scores = (
        jnp.einsum("qhd,khd->qhk", query_rows, key_rows, preferred_element_type=jnp.float32) * scale
    )
    visible = (query_pos[:, None] >= key_pos[None, :]) & (query_docs[:, None] == key_docs[None, :])
    visible = visible[:, None, :]
    scores = jnp.where(visible, scores, masked_score)
    new_top = jnp.maximum(top, jnp.max(scores, axis=2))
    weights = jnp.where(visible, jnp.exp(scores - new_top[:, :, None]), 0.0)
    total = jnp.sum(weights, axis=2)
    update = jnp.einsum(
        "qhk,khd->qhd", weights.astype(jnp.bfloat16), value_rows, preferred_element_type=jnp.float32
    )
    accum = update
    return (new_top, total, accum)


def reduce_pre(partial_pre, live):
    summed = lax.psum(partial_pre.astype(jnp.bfloat16), "mp").astype(jnp.float32)
    active = jnp.where(live[None, :], jnp.maximum(summed, 0.0), 0.0)
    column_sums = jnp.sum(active, axis=0)
    active_low = active.astype(jnp.bfloat16)
    return (active_low, column_sums)


def local(
    resid, queries, keys, values, doc_ids, out_proj, ffn_gain, w_in, w_out, hot_index, hot_blocks
):
    tok_dev = resid.shape[0]
    width_dev = resid.shape[1]
    local_heads = width_dev // HEAD_DIM
    groups = lax.axis_size("seq")
    here = lax.axis_index("seq")
    total_tokens = tok_dev * groups
    scale = HEAD_DIM ** (-0.5)
    doc_table = lax.all_gather(doc_ids, "seq", axis=0, tiled=True)
    positions = here * tok_dev + jnp.arange(tok_dev, dtype=jnp.int32)
    query_rows = queries.reshape(tok_dev, local_heads, HEAD_DIM)
    blocks = (query_rows, positions)
    start_state = []
    block_rows, block_pos = blocks
    count_rows = block_rows.shape[0]
    block_docs = lax.dynamic_slice_in_dim(doc_table, block_pos[0], count_rows)
    query_sets = [(block_rows, block_pos, block_docs)]
    start_state.append(
        (
            jnp.full((count_rows, local_heads), masked_score, jnp.float32),
            jnp.zeros((count_rows, local_heads), jnp.float32),
            jnp.zeros((count_rows, local_heads, HEAD_DIM), jnp.float32),
        )
    )
    start_state = tuple(start_state)
    start = jnp.int32(0)
    key_piece = lax.all_gather(keys, "seq", axis=0, tiled=True)
    value_piece = lax.all_gather(values, "seq", axis=0, tiled=True)
    count = key_piece.shape[0]
    key_rows = key_piece.reshape(count, local_heads, HEAD_DIM)
    value_rows = value_piece.reshape(count, local_heads, HEAD_DIM)
    key_pos = jnp.arange(count, dtype=jnp.int32)
    updated = []
    for fold_state, query_set in zip(start_state, query_sets):

        def visit(current, query_set=query_set):
            return attend_block(
                current,
                query_set[0],
                query_set[1],
                query_set[2],
                key_rows,
                value_rows,
                key_pos,
                doc_table,
                scale,
            )

        def keep(current):
            return current

        updated.append(lax.cond(start <= jnp.max(query_set[1]), visit, keep, fold_state))
    final = tuple(updated)
    outputs = []
    for state in final:
        count_rows = state[2].shape[0]
        outputs.append(
            (state[2] / state[1][:, :, None]).astype(jnp.bfloat16).reshape(count_rows, width_dev)
        )
    attended = outputs[0]
    projected = jnp.dot(attended, out_proj, preferred_element_type=jnp.float32)
    projected = lax.psum_scatter(
        projected.astype(jnp.bfloat16), "mp", scatter_dimension=1, tiled=True
    ).astype(jnp.float32)
    state_rows = (resid.astype(jnp.float32) + projected).astype(jnp.bfloat16)
    widened = state_rows.astype(jnp.float32)
    squares = lax.psum(jnp.sum(widened * widened, axis=1), "mp")
    inverse = lax.rsqrt(squares / D + epsilon)
    normed = (widened * inverse[:, None] * ffn_gain.astype(jnp.float32)).astype(jnp.bfloat16)
    chosen = hot_index[0]
    slots = chosen.shape[0]
    hot_in = jnp.take(w_in, chosen, axis=1)
    hot_out = jnp.take(w_out, chosen, axis=0)
    live = jnp.arange(slots, dtype=jnp.int32) < BLOCK * hot_blocks[0]
    partial_pre = jnp.dot(
        lax.all_gather(normed, "seq", axis=0, tiled=True),
        hot_in,
        preferred_element_type=jnp.float32,
    )
    active_low, column_sums = reduce_pre(partial_pre, live)
    hot_mean = (column_sums / total_tokens)[None, :]
    ffn_out = lax.psum_scatter(
        jnp.dot(active_low, hot_out, preferred_element_type=jnp.float32).astype(jnp.bfloat16),
        "seq",
        scatter_dimension=0,
        tiled=True,
    ).astype(jnp.float32)
    layer_out = (widened + ffn_out).astype(jnp.bfloat16)
    return (layer_out, hot_mean)


def solution(mesh):
    return jax.shard_map(
        local,
        mesh=mesh,
        in_specs=(
            P("seq", "mp"),
            P("seq", "mp"),
            P("seq", "mp"),
            P("seq", "mp"),
            P("seq"),
            P("mp", None),
            P("mp"),
            P("mp", "seq"),
            P("seq", "mp"),
            P("seq", None),
            P("seq"),
        ),
        out_specs=(P("seq", "mp"), P("seq", None)),
        check_vma=False,
    )
```

profile of v0, /device:TPU:0, one launch (start us, length us, event | category | flops | bytes accessed | tf_op | source)
XLA Modules:
  0.0 534.4 jit_solution(12173834518371259901)
XLA Ops:
  7.2 2.2 copy.32
  9.4 2.2 copy.33
  11.7 0.6 fusion.28
  13.0 22.8 %all-gather = s32[8,1,256]{2,1,0:T(1,128)S(1)} all-gather(s32[1,1,256]{2,1,0:T(1,128)} %bitcast.35), channel_id=1, replica_groups=mesh['seq'=8,'mp'=4] {'seq'}, dimensions={0}, use_global_device_ids=true | all-gather | bytes 9216 | tf_op jit(solution)/shard_map/all_gather | solution.py:53
  35.8 64.4 %all-gather.5.cloned.1.call-done = bf16[2048,1280]{0,1:T(8,128)(2,1)} async-done(((bf16[256,1280]{0,1:T(8,128)(2,1)}), bf16[2048,1280]{0,1:T(8,128)(2,1)}) %all-gather.5.cloned.1.call-update) | async-done | bytes 5242896 | tf_op jit(solution)/shard_map/all_gather | solution.py:71
  100.2 87.0 %all-gather.7.cloned.1.call-done = bf16[2048,1280]{0,1:T(8,128)(2,1)} async-done(((bf16[256,1280]{0,1:T(8,128)(2,1)}), bf16[2048,1280]{0,1:T(8,128)(2,1)}) %all-gather.7.cloned.1.call-update) | async-done | bytes 5242896 | tf_op jit(solution)/shard_map/all_gather | solution.py:72
  187.2 41.7 %conditional.1 = (f32[256,10]{0,1:T(8,128)S(1)}, f32[256,10,128]{0,2,1:T(8,128)S(1)}) conditional(s32[]{:T(128)} %convert_element_type.51, () %tuple.23, (s32[256]{0:T(256)S(1)}, s32[2048]{0:T(1024)S(1)}, s32[2048]{0:T(1024)S(1)}, bf16[2048,1280]{0,1:T(8,128)(2,1)}, bf16[256,1280]{1,0:T(8,128)(2,1)}, /*index=5*/bf16[2048,1280]{0,1:T(8,128)(2,1)}) %tuple.45), branch_computations={%region_1.0_spmd, %region_2.5_spmd} | conditional | flops 2754082304 | bytes 81477696 | solution.py:96
  187.2 0.5 slice.4
  189.8 1.4 compare_and_fusion
  191.2 1.3 copy.34
  192.5 13.4 %fusion = (f32[256,10]{0,1:T(8,128)S(1)}, f32[10,2048,256]{2,1,0:T(8,128)}) fusion(pred[256,2048]{0,1:T(8,128)(4,1)S(1)} %compare_and_fusion, bf16[2048,10,128]{0,2,1:T(8,128)(2,1)} %bitcast.31, bf16[256,10,128]{0,2,1:T(8,128)(2,1)S(1)} %bitcast.33), kind=kOutput, calls=%fused_computation.4 | convolution fusion | flops 1357903360 | bytes 27404288 | tf_op jit(solution)/shard_map/cond/branch_1_fun/qhd,khd->qhk/dot_general | solution.py:20
  205.9 10.0 %fusion.2 = f32[256,10]{0,1:T(8,128)S(1)} fusion(f32[10,2048,256]{2,1,0:T(8,128)} %get-tuple-element.95, f32[256,10]{0,1:T(8,128)S(1)} %broadcast_maximum_fusion, pred[256,2048]{0,1:T(8,128)(4,1)S(1)} %compare_and_fusion), kind=kLoop, calls=%fused_computation.6 | loop fusion | flops 26211840 | bytes 21516288 | tf_op jit(solution)/shard_map/cond/branch_1_fun/reduce_sum | solution.py:27
  215.9 12.5 %fusion.6 = f32[256,10,128]{2,0,1:T(8,128)S(1)} fusion(bf16[2048,10,128]{0,2,1:T(8,128)(2,1)} %bitcast.36, f32[10,2048,256]{2,1,0:T(8,128)} %get-tuple-element.95, f32[256,10]{0,1:T(8,128)S(1)} %broadcast_maximum_fusion, pred[256,2048]{0,1:T(8,128)(4,1)S(1)} %compare_and_fusion), kind=kOutput, calls=%fused_computation.10 | convolution fusion | flops 1368391680 | bytes 28059648 | tf_op jit(solution)/shard_map/cond/branch_1_fun/qhk,khd->qhd/dot_general | solution.py:28
  228.4 0.4 copy.41
  229.0 0.1 divide_convert_fusion
  229.1 9.8 %convolution_convert_fusion.1 = bf16[256,5120]{1,0:T(8,128)(2,1)} fusion(bf16[256,1280]{0,1:T(8,128)(2,1)S(1)} %bitcast.32, bf16[1280,5120]{1,0:T(8,128)(2,1)} %param.18), kind=kOutput, calls=%fused_computation.16 | convolution fusion | flops 3356753920 | bytes 16384000 | tf_op jit(solution)/shard_map/dot_general | solution.py:105
  239.0 32.6 %reduce-scatter.3.cloned.1.call-done = bf16[256,1280]{1,0:T(8,128)(2,1)} async-done(((bf16[256,5120]{1,0:T(8,128)(2,1)}), bf16[256,1280]{1,0:T(8,128)(2,1)}) %reduce-scatter.3.cloned.1.call-update) | async-done | bytes 655376 | tf_op jit(solution)/shard_map/reduce_scatter | solution.py:106
  271.7 1.4 fusion.17
  273.0 5.8 %psum.14 = f32[256]{0:T(256)S(1)} all-reduce(f32[256]{0:T(256)S(1)} %fusion.17), channel_id=1, replica_groups=mesh['seq'=8,'mp'=4] {'mp'}, use_global_device_ids=true, to_apply=%region_7.8 | all-reduce | flops 256 | bytes 2048 | tf_op jit(solution)/shard_map/psum | solution.py:111
  278.8 2.2 fusion.19
  281.1 6.0 %gather_fusion = bf16[384,1280]{1,0:T(8,128)(2,1)S(1)} fusion(bf16[1280,1728]{0,1:T(8,128)(2,1)} %param.20, s32[1024]{0:T(1024)S(1)} %pad_clamp_fusion), kind=kCustom, calls=%fused_computation | custom fusion | bytes 1967616 | tf_op jit(solution)/shard_map/jit(_take)/gather | solution.py:116
  287.2 80.5 %all-gather.9.cloned.1.call-done = bf16[2048,1280]{1,0:T(8,128)(2,1)} async-done(((bf16[256,1280]{1,0:T(8,128)(2,1)}), bf16[2048,1280]{1,0:T(8,128)(2,1)}) %all-gather.9.cloned.1.call-update) | async-done | bytes 5242896 | tf_op jit(solution)/shard_map/all_gather | solution.py:120
  367.6 6.6 %convolution_convert_fusion.2 = bf16[2048,384]{1,0:T(8,128)(2,1)} fusion(bf16[2048,1280]{1,0:T(8,128)(2,1)} %all-gather.9.cloned.1.call-done, bf16[384,1280]{1,0:T(8,128)(2,1)S(1)} %gather_fusion, pred[384]{0:T(512)(128)(4,1)S(1)} %compare_and_fusion.1), kind=kOutput, calls=%fused_computation.20 | convolution fusion | flops 2014543872 | bytes 7799168 | tf_op jit(solution)/shard_map/dot_general | solution.py:119
  374.3 0.3 reduce-scatter.5.cloned.1.call-start
  375.2 6.0 %gather_fusion.1 = bf16[384,1280]{1,0:T(8,128)(2,1)S(1)} fusion(bf16[1728,1280]{1,0:T(8,128)(2,1)} %param.21, s32[1024]{0:T(1024)S(1)} %pad_clamp_fusion), kind=kCustom, calls=%fused_computation.1 | custom fusion | bytes 1967616 | tf_op jit(solution)/shard_map/jit(_take)/gather | solution.py:117
  381.3 34.2 %all-reduce.2.cloned.1.call-done = bf16[2048,384]{1,0:T(8,128)(2,1)} async-done(((bf16[2048,384]{1,0:T(8,128)(2,1)}), bf16[2048,384]{1,0:T(8,128)(2,1)}) %all-reduce.2.cloned.1.call-update) | async-done | bytes 1572880 | tf_op jit(solution)/shard_map/psum | solution.py:36
  415.5 6.7 %convolution_convert_fusion = bf16[2048,1280]{1,0:T(8,128)(2,1)} fusion(bf16[2048,384]{1,0:T(8,128)(2,1)} %all-reduce.2.cloned.1.call-done, pred[384]{0:T(512)(128)(4,1)S(1)} %iota_compare_fusion, bf16[384,1280]{1,0:T(8,128)(2,1)S(1)} %gather_fusion.1, pred[384]{0:T(512)(128)(4,1)S(1)} %compare_and_fusion.1), kind=kOutput, calls=%fused_computation.15 | convolution fusion | flops 2019524608 | bytes 7799552 | tf_op jit(solution)/shard_map/dot_general | solution.py:127
  422.2 1.4 copy-done.2
  423.6 0.5 fusion.12
  424.1 0.6 div.28
  424.7 100.7 %reduce-scatter.5.cloned.1.call-done = bf16[256,1280]{1,0:T(8,128)(2,1)} async-done(((bf16[2048,1280]{1,0:T(8,128)(2,1)}), bf16[256,1280]{1,0:T(8,128)(2,1)}) %reduce-scatter.5.cloned.1.call-update) | async-done | bytes 655376 | tf_op jit(solution)/shard_map/reduce_scatter | solution.py:126
  525.4 2.2 fusion.20
  (32 shorter events, 0.5 us)
Async XLA Ops:
  7.2 93.0 %all-gather.5.cloned.1.call-start = ((), (), s32[]{:S(2)}) async-start(), calls=%async_computation.2 | async-start | bytes 5898240 | tf_op jit(solution)/shard_map/all_gather | solution.py:71
  9.4 177.8 %all-gather.7.cloned.1.call-start = ((), (), s32[]{:S(2)}) async-start(), calls=%async_computation.3 | async-start | bytes 5898240 | tf_op jit(solution)/shard_map/all_gather | solution.py:72
  11.6 260.0 %reduce-scatter.3.cloned.1.call-start = ((), (), s32[]{:S(2)}) async-start(), calls=%async_computation.4 | async-start | bytes 3276800 | tf_op jit(solution)/shard_map/reduce_scatter | solution.py:106
  229.1 9.9 %copy-start.4 = (bf16[1280]{0:T(1024)(128)(2,1)S(1)}, bf16[1280]{0:T(1024)(128)(2,1)}, u32[]{:S(2)}) copy-start(bf16[1280]{0:T(1024)(128)(2,1)} %param.19) | copy-start | bytes 7684
  229.1 42.5 %copy-start = (bf16[256,1280]{1,0:T(8,128)(2,1)S(1)}, bf16[256,1280]{1,0:T(8,128)(2,1)}, u32[]{:S(2)}) copy-start(bf16[256,1280]{1,0:T(8,128)(2,1)} %param.13) | copy-start | bytes 1966084
  238.9 42.1 %copy-start.3 = (s32[1,384]{1,0:T(1,128)S(1)}, s32[1,384]{1,0:T(1,128)}, u32[]{:S(2)}) copy-start(s32[1,384]{1,0:T(1,128)} %param.22) | copy-start | bytes 4612
  238.9 128.7 %all-gather.9.cloned.1.call-start = ((), (), s32[]{:S(2)}) async-start(), calls=%async_computation.5 | async-start | bytes 5898240 | tf_op jit(solution)/shard_map/all_gather | solution.py:120
  281.0 134.5 %all-reduce.2.cloned.1.call-start = ((), (), s32[]{:S(2)}) async-start(), calls=%async_computation.6 | async-start | bytes 3145728 | tf_op jit(solution)/shard_map/psum | solution.py:36
  374.3 151.1 %reduce-scatter.5.cloned.1.call-start = ((), (), s32[]{:S(2)}) async-start(), calls=%async_computation.7 | async-start | bytes 5898240 | tf_op jit(solution)/shard_map/reduce_scatter | solution.py:126
  422.2 1.4 copy-start.2
  422.2 103.2 %copy-start.1 = (bf16[256,1280]{1,0:T(8,128)(2,1)S(1)}, bf16[256,1280]{1,0:T(8,128)(2,1)}, u32[]{:S(2)}) copy-start(bf16[256,1280]{1,0:T(8,128)(2,1)} %reduce-scatter.3.cloned.1.call-done) | copy-start | bytes 1966084
Sparse Core Ops, SparseCore 0:
  10.6 89.5 all-gather.4
  102.2 84.9 all-gather.6
  239.1 32.5 reduce-scatter.2
  281.1 86.4 all-gather.8
  374.4 41.0 all-reduce.1
  422.4 103.0 reduce-scatter.4
where the time goes:
time: 535 us; the launch traced here: 534 us
  waiting for transfers between devices  400 us (75%)
  matrix products  49 us (9%)
  blocking collectives  28.5 us (5%)
  local copies, waits for them, and re-layouts  20.7 us (4%)
  other arithmetic  18.5 us (3%)
  between operations  15.5 us (3%)
    reduce_scatter x1, waiting for transfers between devices, local(): lax.psum_scatter(jnp.dot(active_low, hot_out, preferred_element_type=jnp....  101 us
    all_gather x1, waiting for transfers between devices, local(): value_piece = lax.all_gather(values, 'seq', axis=0, tiled=True)  87 us
    all_gather x1, waiting for transfers between devices, local(): lax.all_gather(normed, 'seq', axis=0, tiled=True)  80.5 us
    all_gather x1, waiting for transfers between devices, local(): key_piece = lax.all_gather(keys, 'seq', axis=0, tiled=True)  64.4 us
    psum x1, waiting for transfers between devices, reduce_pre(): lax.psum(partial_pre.astype(jnp.bfloat16), 'mp').astype(jnp.float32)  34.2 us
    reduce_scatter x1, waiting for transfers between devices, local(): lax.psum_scatter(projected.astype(jnp.bfloat16), 'mp', scatter_dimension=...  32.6 us
    all_gather x1, blocking collectives, local(): doc_table = lax.all_gather(doc_ids, 'seq', axis=0, tiled=True)  22.8 us
    dot_general x1, matrix products, attend_block(): jnp.einsum('qhd,khd->qhk', query_rows, key_rows, preferred_element_type=j...  13.4 us
  transfers between devices with their start and end apart: 6, of which 6 were waited for; matrix products, arithmetic and copies ran while one was open for 3% of the time, Pallas kernels for 0%

commit v1 on v0

v1 whole, which is shorter than its diff:
```python
import functools

import jax
import jax.numpy as jnp
from jax import lax
from jax.experimental import pallas as pl
from jax.experimental.pallas import tpu as pltpu
from jax.sharding import PartitionSpec as P

HEAD_DIM = 128
BLOCK = 128
MESH = pl.DeviceIdType.MESH
VMEM = pltpu.VMEM

epsilon = 1e-05
masked_score = -1e30


def row_length(mesh):
    seq = mesh.shape["seq"]
    try:
        first = [mesh.devices[i, 0].coords for i in range(seq)]
        size = len({c[1] for c in first})
        if seq % size == 0:
            return size
    except (AttributeError, IndexError, TypeError):
        pass
    return 2


def gather_kernel(nz, ny, up, down, window, chunks, count, *refs):
    ins = refs[:count]
    outs = refs[count : 2 * count]
    sems = refs[2 * count :]
    own_sem, zs_sem, zr_sem, ys_sem, yr_sem = sems
    me = lax.axis_index("seq")
    mp = lax.axis_index("mp")
    z = me // ny
    y = me % ny

    def dev(zz, yy):
        return (zz * ny + yy, mp)

    barrier = pltpu.get_barrier_semaphore()
    for step in (-1, 1):
        ok = (z + step >= 0) & (z + step < nz)

        @pl.when(ok)
        def _(step=step):
            pl.semaphore_signal(barrier, inc=1, device_id=dev(z + step, y), device_id_type=MESH)

    for dy in range(1, ny):
        pl.semaphore_signal(
            barrier, inc=1, device_id=dev(z, (y + dy) % ny), device_id_type=MESH
        )
    below = jnp.where(z > 0, 1, 0)
    above = jnp.where(z < nz - 1, 1, 0)
    pl.semaphore_wait(barrier, below + above + ny - 1)

    def piece(ref, a, c):
        rows = ins[a].shape[0]
        if chunks[a] == 1:
            return ref
        size = rows // chunks[a]
        return ref.at[pl.ds(c * size, size)]

    def slot(a, zz, yy, c):
        return piece(outs[a].at[zz * ny + yy], a, c)

    base = []
    total = 0
    for a in range(count):
        base.append(total)
        total += chunks[a]

    def own_copy(a):
        return pltpu.make_async_copy(ins[a], outs[a].at[me], own_sem.at[a])

    def level_z(lv):
        return z - lv if lv <= up else z + (lv - up)

    def source(lv, a, c):
        if lv == 0:
            return piece(ins[a], a, c)
        return slot(a, level_z(lv), y, c)

    def z_copy(lv, direction, a, c):
        there = (lv + 1) if direction > 0 else (up + 1 if lv == 0 else lv + 1)
        return pltpu.make_async_remote_copy(
            src_ref=source(lv, a, c),
            dst_ref=slot(a, level_z(lv), y, c),
            send_sem=zs_sem.at[there - 1, base[a] + c],
            recv_sem=zr_sem.at[there - 1, base[a] + c],
            device_id=dev(z + direction, y),
            device_id_type=MESH,
        )

    def z_cond(lv, direction):
        src = level_z(lv)
        return (src >= 0) & (src < nz) & (z + direction >= 0) & (z + direction < nz)

    def y_needed(lv, y_from, y_to):
        src = level_z(lv)
        ok = (src >= 0) & (src < nz)
        if window is not None:
            offset = (z - src) * ny + y_to - y_from
            ok = ok & (offset >= 0) & (offset <= window)
        return ok

    def y_copy(lv, dy, a, c):
        return pltpu.make_async_remote_copy(
            src_ref=source(lv, a, c),
            dst_ref=slot(a, level_z(lv), y, c),
            send_sem=ys_sem.at[lv * (ny - 1) + dy - 1, base[a] + c],
            recv_sem=yr_sem.at[lv * (ny - 1) + dy - 1, base[a] + c],
            device_id=dev(z, (y + dy) % ny),
            device_id_type=MESH,
        )

    def y_arrival(lv, dy, a, c):
        return pltpu.make_async_remote_copy(
            src_ref=source(lv, a, c),
            dst_ref=slot(a, level_z(lv), (y + ny - dy) % ny, c),
            send_sem=ys_sem.at[lv * (ny - 1) + dy - 1, base[a] + c],
            recv_sem=yr_sem.at[lv * (ny - 1) + dy - 1, base[a] + c],
            device_id=dev(z, (y + dy) % ny),
            device_id_type=MESH,
        )

    every = [(a, c) for a in range(count) for c in range(chunks[a])]

    def directions(lv):
        out = []
        if lv < up:
            out.append(1)
        if down and (lv == 0 or (lv > up and lv - up < down)):
            out.append(-1)
        return out

    def spread(lv, a, c):
        for direction in directions(lv):

            @pl.when(z_cond(lv, direction))
            def _(direction=direction):
                z_copy(lv, direction, a, c).start()

        for dy in range(1, ny):

            @pl.when(y_needed(lv, y, (y + dy) % ny))
            def _(dy=dy):
                y_copy(lv, dy, a, c).start()

    for a, c in every:
        spread(0, a, c)
    for a in range(count):
        own_copy(a).start()
    order = []
    for k in range(1, max(up, down) + 1):
        for a, c in every:
            if k <= up:
                order.append((k, a, c))
            if k <= down:
                order.append((up + k, a, c))
    for lv, a, c in order:
        src = level_z(lv)

        @pl.when((src >= 0) & (src < nz))
        def _(lv=lv, a=a, c=c):
            pltpu.make_async_remote_copy(
                src_ref=slot(a, level_z(lv), y, c),
                dst_ref=slot(a, level_z(lv), y, c),
                send_sem=zs_sem.at[lv - 1, base[a] + c],
                recv_sem=zr_sem.at[lv - 1, base[a] + c],
                device_id=dev(z, (y + 1) % ny),
                device_id_type=MESH,
            ).wait_recv()
            spread(lv, a, c)

    for lv in range(up + down + 1):
        for a, c in every:
            for dy in range(1, ny):

                @pl.when(y_needed(lv, (y + ny - dy) % ny, y))
                def _(lv=lv, a=a, c=c, dy=dy):
                    y_arrival(lv, dy, a, c).wait_recv()

    for lv in range(up + down + 1):
        for a, c in every:
            for direction in directions(lv):

                @pl.when(z_cond(lv, direction))
                def _(lv=lv, a=a, c=c, direction=direction):
                    z_copy(lv, direction, a, c).wait_send()

            for dy in range(1, ny):

                @pl.when(y_needed(lv, y, (y + dy) % ny))
                def _(lv=lv, a=a, c=c, dy=dy):
                    y_copy(lv, dy, a, c).wait_send()

    for a in range(count):
        own_copy(a).wait()


def seq_gather(arrays, ny, causal, chunks, collective_id):
    n = lax.axis_size("seq")
    nz = n // ny
    if causal:
        window = n // 2
        up, down = min(nz - 1, -(-window // ny)), 0
    else:
        window = None
        up = down = nz - 1
    count = len(arrays)
    total = sum(chunks)
    levels = up + down
    return pl.pallas_call(
        functools.partial(gather_kernel, nz, ny, up, down, window, chunks, count),
        out_shape=[jax.ShapeDtypeStruct((n,) + a.shape, a.dtype) for a in arrays],
        in_specs=[pl.BlockSpec(memory_space=VMEM)] * count,
        out_specs=[pl.BlockSpec(memory_space=pl.ANY)] * count,
        scratch_shapes=[
            pltpu.SemaphoreType.DMA((count,)),
            pltpu.SemaphoreType.DMA((levels, total)),
            pltpu.SemaphoreType.DMA((levels, total)),
            pltpu.SemaphoreType.DMA(((levels + 1) * (ny - 1), total)),
            pltpu.SemaphoreType.DMA(((levels + 1) * (ny - 1), total)),
        ],
        compiler_params=pltpu.CompilerParams(
            collective_id=collective_id, has_side_effects=True
        ),
    )(*arrays)


def attention_kernel(window, scale, q_ref, k_ref, v_ref, qdoc_ref, kdoc_ref, out_ref):
    here = lax.axis_index("seq")
    rows = q_ref.shape[0]
    query = q_ref[...]
    query_doc = qdoc_ref[...]
    row = lax.broadcasted_iota(jnp.int32, (rows, rows), 0)
    col = lax.broadcasted_iota(jnp.int32, (rows, rows), 1)
    first = jnp.maximum(here - window, 0)

    def visit(block, carry):
        top, total, accum = carry
        scores = (
            lax.dot_general(
                query,
                k_ref[block],
                (((1,), (1,)), ((), ())),
                preferred_element_type=jnp.float32,
            )
            * scale
        )
        visible = (query_doc == kdoc_ref[block, 0:1, :]) & (
            row - col >= (block - here) * rows
        )
        scores = jnp.where(visible, scores, masked_score)
        new_top = jnp.maximum(top, jnp.max(scores, axis=1, keepdims=True))
        weights = jnp.where(visible, jnp.exp(scores - new_top), 0.0)
        fade = jnp.exp(top - new_top)
        total = total * fade + jnp.sum(weights, axis=1, keepdims=True)
        accum = accum * fade + jnp.dot(
            weights.astype(jnp.bfloat16), v_ref[block], preferred_element_type=jnp.float32
        )
        return new_top, total, accum

    start = (
        jnp.full((rows, 1), masked_score, jnp.float32),
        jnp.zeros((rows, 1), jnp.float32),
        jnp.zeros((rows, HEAD_DIM), jnp.float32),
    )
    _, total, accum = lax.fori_loop(first, here + 1, visit, start)
    out_ref[...] = (accum / total).astype(jnp.bfloat16)


def attention(queries, keys, values, doc_col, doc_rows):
    rows, width = queries.shape
    n = keys.shape[0]
    heads = width // HEAD_DIM
    return pl.pallas_call(
        functools.partial(attention_kernel, n // 2, HEAD_DIM ** (-0.5)),
        grid=(heads,),
        out_shape=jax.ShapeDtypeStruct((rows, width), jnp.bfloat16),
        in_specs=[
            pl.BlockSpec((rows, HEAD_DIM), lambda h: (0, h)),
            pl.BlockSpec((n, rows, HEAD_DIM), lambda h: (0, 0, h)),
            pl.BlockSpec((n, rows, HEAD_DIM), lambda h: (0, 0, h)),
            pl.BlockSpec((rows, 1), lambda h: (0, 0)),
            pl.BlockSpec(doc_rows.shape, lambda h: (0, 0, 0)),
        ],
        out_specs=pl.BlockSpec((rows, HEAD_DIM), lambda h: (0, h)),
    )(queries, keys, values, doc_col, doc_rows)


def mp_scatter_kernel(n, x_ref, out_ref, near, sums, far, s1, r1, s2, r2):
    seq = lax.axis_index("seq")
    me = lax.axis_index("mp")
    chips = n // 2
    chip = me // 2
    core = me % 2
    partner = chip * 2 + 1 - core
    width = out_ref.shape[1]
    barrier = pltpu.get_barrier_semaphore()
    pl.semaphore_signal(barrier, inc=1, device_id=(seq, partner), device_id_type=MESH)
    for d in range(1, chips):
        other = ((chip + d) % chips) * 2 + core
        pl.semaphore_signal(barrier, inc=1, device_id=(seq, other), device_id_type=MESH)
    pl.semaphore_wait(barrier, chips)

    def columns(index):
        return pl.ds(pl.multiple_of(index * width, 128), width)

    first = []
    for d in list(range(1, chips)) + [0]:
        target = (chip + d) % chips
        copy = pltpu.make_async_remote_copy(
            src_ref=x_ref.at[:, columns(target * 2 + 1 - core)],
            dst_ref=near.at[d],
            send_sem=s1.at[d],
            recv_sem=r1.at[d],
            device_id=(seq, partner),
            device_id_type=MESH,
        )
        copy.start()
        first.append((d, target, copy))
    second = []
    for d, target, copy in first:
        copy.wait_recv()
        mine = x_ref[:, columns(target * 2 + core)].astype(jnp.float32)
        total = mine + near[d].astype(jnp.float32)
        if d == 0:
            out_ref[...] = total
            continue
        sums[d - 1] = total.astype(jnp.bfloat16)
        send = pltpu.make_async_remote_copy(
            src_ref=sums.at[d - 1],
            dst_ref=far.at[d - 1],
            send_sem=s2.at[d - 1],
            recv_sem=r2.at[d - 1],
            device_id=(seq, target * 2 + core),
            device_id_type=MESH,
        )
        send.start()
        second.append((d, send))
    for d, send in second:
        send.wait_recv()
        out_ref[...] += far[d - 1].astype(jnp.float32)
    for d, target, copy in first:
        copy.wait_send()
    for d, send in second:
        send.wait_send()


def mp_scatter(x, collective_id):
    n = lax.axis_size("mp")
    rows, total = x.shape
    width = total // n
    chips = n // 2
    return pl.pallas_call(
        functools.partial(mp_scatter_kernel, n),
        out_shape=jax.ShapeDtypeStruct((rows, width), jnp.float32),
        in_specs=[pl.BlockSpec(memory_space=VMEM)],
        out_specs=pl.BlockSpec(memory_space=VMEM),
        scratch_shapes=[
            VMEM((chips, rows, width), jnp.bfloat16),
            VMEM((chips - 1, rows, width), jnp.bfloat16),
            VMEM((chips - 1, rows, width), jnp.bfloat16),
            pltpu.SemaphoreType.DMA((chips,)),
            pltpu.SemaphoreType.DMA((chips,)),
            pltpu.SemaphoreType.DMA((chips - 1,)),
            pltpu.SemaphoreType.DMA((chips - 1,)),
        ],
        compiler_params=pltpu.CompilerParams(
            collective_id=collective_id, has_side_effects=True, vmem_limit_bytes=48 * 1024 * 1024
        ),
    )(x)


def seq_scatter_kernel(nz, ny, x_ref, out_ref, near, sums, far, s1, r1, s2, r2):
    me = lax.axis_index("seq")
    mp = lax.axis_index("mp")
    z = me // ny
    y = me % ny
    barrier = pltpu.get_barrier_semaphore()
    for d in range(1, ny):
        peer = z * ny + (y + d) % ny
        pl.semaphore_signal(barrier, inc=1, device_id=(peer, mp), device_id_type=MESH)
    for d in range(1, nz):
        peer = ((z + d) % nz) * ny + y
        pl.semaphore_signal(barrier, inc=1, device_id=(peer, mp), device_id_type=MESH)
    pl.semaphore_wait(barrier, ny + nz - 2)

    first = []
    for d in list(range(1, nz)) + [0]:
        target = (z + d) % nz
        group = []
        for e in range(1, ny):
            other = (y + e) % ny
            copy = pltpu.make_async_remote_copy(
                src_ref=x_ref.at[target * ny + other],
                dst_ref=near.at[d, e - 1],
                send_sem=s1.at[d, e - 1],
                recv_sem=r1.at[d, e - 1],
                device_id=(z * ny + other, mp),
                device_id_type=MESH,
            )
            copy.start()
            group.append(copy)
        first.append((d, target, group))
    second = []
    for d, target, group in first:
        total = x_ref[target * ny + y].astype(jnp.float32)
        for e, copy in enumerate(group):
            copy.wait_recv()
            total = total + near[d, e].astype(jnp.float32)
        if d == 0:
            out_ref[...] = total
            continue
        sums[d - 1] = total.astype(jnp.bfloat16)
        send = pltpu.make_async_remote_copy(
            src_ref=sums.at[d - 1],
            dst_ref=far.at[d - 1],
            send_sem=s2.at[d - 1],
            recv_sem=r2.at[d - 1],
            device_id=(target * ny + y, mp),
            device_id_type=MESH,
        )
        send.start()
        second.append((d, send))
    for d, send in second:
        send.wait_recv()
        out_ref[...] += far[d - 1].astype(jnp.float32)
    for d, target, group in first:
        for copy in group:
            copy.wait_send()
    for d, send in second:
        send.wait_send()


def seq_scatter(x, ny, collective_id):
    n, rows, width = x.shape
    nz = n // ny
    dma = pltpu.SemaphoreType.DMA
    return pl.pallas_call(
        functools.partial(seq_scatter_kernel, nz, ny),
        out_shape=jax.ShapeDtypeStruct((rows, width), jnp.float32),
        in_specs=[pl.BlockSpec(memory_space=VMEM)],
        out_specs=pl.BlockSpec(memory_space=VMEM),
        scratch_shapes=[
            VMEM((nz, ny - 1, rows, width), jnp.bfloat16),
            VMEM((nz - 1, rows, width), jnp.bfloat16),
            VMEM((nz - 1, rows, width), jnp.bfloat16),
            dma((nz, ny - 1)),
            dma((nz, ny - 1)),
            dma((nz - 1,)),
            dma((nz - 1,)),
        ],
        compiler_params=pltpu.CompilerParams(
            collective_id=collective_id, has_side_effects=True, vmem_limit_bytes=48 * 1024 * 1024
        ),
    )(x)


def reduce_pre(partial_pre, live):
    summed = lax.psum(partial_pre.astype(jnp.bfloat16), "mp").astype(jnp.float32)
    active = jnp.where(live[None, :], jnp.maximum(summed, 0.0), 0.0)
    column_sums = jnp.sum(active, axis=0)
    return (active.astype(jnp.bfloat16), column_sums)


def local(
    ny,
    resid,
    queries,
    keys,
    values,
    doc_ids,
    out_proj,
    ffn_gain,
    w_in,
    w_out,
    hot_index,
    hot_blocks,
):
    tok_dev, width_dev = resid.shape
    groups = lax.axis_size("seq")
    width = width_dev * lax.axis_size("mp")
    total_tokens = tok_dev * groups
    doc_row = jnp.broadcast_to(doc_ids[None, :], (8, tok_dev))
    doc_rows, all_keys, all_values = seq_gather(
        [doc_row, keys, values], ny, True, (1, 2, 2), 0
    )
    chosen = hot_index[0]
    slots = chosen.shape[0]
    hot_in = jnp.take(w_in, chosen, axis=1)
    hot_out = jnp.take(w_out, chosen, axis=0)
    live = jnp.arange(slots, dtype=jnp.int32) < BLOCK * hot_blocks[0]
    attended = attention(queries, all_keys, all_values, doc_ids[:, None], doc_rows)
    projected = jnp.dot(attended, out_proj, preferred_element_type=jnp.float32)
    projected = mp_scatter(projected.astype(jnp.bfloat16), 1)
    state_rows = (resid.astype(jnp.float32) + projected).astype(jnp.bfloat16)
    widened = state_rows.astype(jnp.float32)
    squares = lax.psum(jnp.sum(widened * widened, axis=1), "mp")
    inverse = lax.rsqrt(squares / width + epsilon)
    normed = (widened * inverse[:, None] * ffn_gain.astype(jnp.float32)).astype(jnp.bfloat16)
    (all_normed,) = seq_gather([normed], ny, False, (4,), 2)
    partial_pre = jnp.dot(
        all_normed.reshape(total_tokens, width_dev),
        hot_in,
        preferred_element_type=jnp.float32,
    )
    active_low, column_sums = reduce_pre(partial_pre, live)
    hot_mean = (column_sums / total_tokens)[None, :]
    contribution = jnp.dot(active_low, hot_out, preferred_element_type=jnp.float32)
    contribution = contribution.astype(jnp.bfloat16).reshape(groups, tok_dev, width_dev)
    ffn_out = seq_scatter(contribution, ny, 3)
    layer_out = (widened + ffn_out).astype(jnp.bfloat16)
    return (layer_out, hot_mean)


def solution(mesh):
    return jax.shard_map(
        functools.partial(local, row_length(mesh)),
        mesh=mesh,
        in_specs=(
            P("seq", "mp"),
            P("seq", "mp"),
            P("seq", "mp"),
            P("seq", "mp"),
            P("seq"),
            P("mp", None),
            P("mp"),
            P("mp", "seq"),
            P("seq", "mp"),
            P("seq", None),
            P("seq"),
        ),
        out_specs=(P("seq", "mp"), P("seq", None)),
        check_vma=False,
    )
```

time: 535 us -> 355 us (0.66)
  waiting for transfers between devices: 400 us -> 44.3 us
  Pallas kernels: 0 us -> 249 us
  matrix products: 49 us -> 21.8 us
  blocking collectives: 28.5 us -> 5.76 us
  other arithmetic: 18.5 us -> 2.86 us
    pallas_call x0 -> x5, Pallas kernels: none -> 249 us  [the longest x2 140 us: seq_gather(): pl.pallas_call(functools.partial(gather_kernel, nz, ny, up, down, window,...]
    all_gather x3 -> x0, waiting for transfers between devices: 232 us -> none  [the longest x1 87 us: local(): value_piece = lax.all_gather(values, 'seq', axis=0, tiled=True)]
    reduce_scatter x2 -> x0, waiting for transfers between devices: 133 us -> none  [the longest x1 101 us: local(): lax.psum_scatter(jnp.dot(active_low, hot_out, preferred_element_type=jnp....]
    dot_general x3 -> x1, matrix products: 32.5 us -> 6.62 us  [local(): jnp.dot(all_normed.reshape(total_tokens, width_dev), hot_in, preferred_el...]
    all_gather x1 -> x0, blocking collectives: 22.8 us -> none  [local(): doc_table = lax.all_gather(doc_ids, 'seq', axis=0, tiled=True)]
    psum x1, waiting for transfers between devices: 34.2 us -> 44.3 us  [reduce_pre(): lax.psum(partial_pre.astype(jnp.bfloat16), 'mp').astype(jnp.float32)]
    reduce_sum x1 -> x0, other arithmetic: 10 us -> none  [attend_block(): total = jnp.sum(weights, axis=2)]
    unnamed x12 -> x8, local copies, waits for them, and re-layouts: 5.73 us -> 0.02 us
  transfers between devices with their start and end apart: 6 -> 1, of which waited for: 6 -> 1; matrix products, arithmetic and copies ran while one was open for 3% -> 2% of each run, Pallas kernels for 0% -> 0%
where the time goes in v1:
time: 355 us; the launch traced here: 354 us
  Pallas kernels  249 us (70%)
  waiting for transfers between devices  44.3 us (12%)
  matrix products  21.8 us (6%)
  local copies, waits for them, and re-layouts  15.4 us (4%)
  between operations  14.8 us (4%)
  blocking collectives  5.76 us (2%)
    pallas_call x2, Pallas kernels, seq_gather(): pl.pallas_call(functools.partial(gather_kernel, nz, ny, up, down, window,...  140 us
    pallas_call x1, Pallas kernels, seq_scatter(): pl.pallas_call(functools.partial(seq_scatter_kernel, nz, ny), out_shape=j...  78.5 us
    psum x1, waiting for transfers between devices, reduce_pre(): lax.psum(partial_pre.astype(jnp.bfloat16), 'mp').astype(jnp.float32)  44.3 us
    pallas_call x1, Pallas kernels, mp_scatter(): pl.pallas_call(functools.partial(mp_scatter_kernel, n), out_shape=jax.Sha...  19.4 us
    pallas_call x1, Pallas kernels, attention(): pl.pallas_call(functools.partial(attention_kernel, n // 2, HEAD_DIM ** (-...  11 us
    dot_general x1, matrix products, local(): projected = jnp.dot(attended, out_proj, preferred_element_type=jnp.float32)  8.5 us
  transfers between devices with their start and end apart: 1, of which 1 were waited for; matrix products, arithmetic and copies ran while one was open for 2% of the time, Pallas kernels for 0%

profile of v1, /device:TPU:0, one launch (start us, length us, event | category | flops | bytes accessed | tf_op | source)
XLA Modules:
  0.0 354.1 jit_solution(15701410376798748848)
XLA Ops:
  7.2 0.0 all-reduce.2.cloned.1.call-start
  7.2 1.5 copy.13.qdoc_ref
  8.7 1.3 broadcast_in_dim.43.refs_0_
  10.0 33.0 %shard_map.122 = (s32[8,8,256]{2,1,0:T(8,128)}, bf16[8,256,1280]{2,1,0:T(8,128)(2,1)}, bf16[8,256,1280]{2,1,0:T(8,128)(2,1)}) custom-call(s32[8,256]{1,0:T(8,128)} %broadcast_in_dim.43.refs_0_, bf16[256,1280]{1,0:T(8,128)(2,1)} %refs_1_.1, bf16[256,1280]{1,0:T(8,128)(2,1)} %refs_2_.1), custom_call_target="tpu_custom_call" | custom-call | tf_op jit(solution)/shard_map/pallas_call | solution.py:217
  43.0 11.0 %shard_map.123 = bf16[256,1280]{1,0:T(8,128)(2,1)} custom-call(bf16[256,1280]{1,0:T(8,128)(2,1)} %q_ref.1, bf16[8,256,1280]{2,1,0:T(8,128)(2,1)} %get-tuple-element.5.k_ref, bf16[8,256,1280]{2,1,0:T(8,128)(2,1)} %get-tuple-element.6.v_ref, s32[256,1]{1,0:T(8,128)} %copy.13.qdoc_ref, s32[8,8,256]{2,1,0:T(8,128)} %get-tuple-element.7.kdoc_ref), custom_call_target="tpu_custom_call" | custom-call | tf_op jit(solution)/shard_map/pallas_call | solution.py:281
  54.0 8.5 %convolution_convert_fusion.1.x_ref = bf16[256,5120]{1,0:T(8,128)(2,1)S(1)} fusion(bf16[256,1280]{1,0:T(8,128)(2,1)} %shard_map.123, bf16[1280,5120]{1,0:T(8,128)(2,1)} %param.16), kind=kOutput, calls=%fused_computation.3 | convolution fusion | flops 3356753920 | bytes 16384000 | tf_op jit(solution)/shard_map/dot_general | solution.py:500
  62.5 0.0 copy-start.1
  62.5 0.0 copy-start.3
  62.5 19.4 %shard_map.124 = f32[256,1280]{1,0:T(8,128)S(1)} custom-call(bf16[256,5120]{1,0:T(8,128)(2,1)S(1)} %convolution_convert_fusion.1.x_ref), custom_call_target="tpu_custom_call" | custom-call | tf_op jit(solution)/shard_map/pallas_call | solution.py:360
  81.9 0.0 copy-done.1
  81.9 0.3 fusion.5
  82.2 5.8 %psum.14 = f32[256]{0:T(256)S(1)} all-reduce(f32[256]{0:T(256)S(1)} %get-tuple-element.8), channel_id=1, replica_groups=mesh['seq'=8,'mp'=4] {'mp'}, use_global_device_ids=true, to_apply=%region_1.2 | all-reduce | flops 256 | bytes 2048 | tf_op jit(solution)/shard_map/psum | solution.py:504
  88.0 0.0 copy-done.3
  88.0 1.1 fusion.7.refs_0_
  89.0 0.0 copy-start.2
  89.0 107.2 %shard_map.125 = bf16[8,256,1280]{2,1,0:T(8,128)(2,1)} custom-call(bf16[256,1280]{1,0:T(8,128)(2,1)} %fusion.7.refs_0_), custom_call_target="tpu_custom_call" | custom-call | tf_op jit(solution)/shard_map/pallas_call | solution.py:217
  196.3 0.0 copy-done.2
  196.4 6.0 %gather_fusion = bf16[384,1280]{1,0:T(8,128)(2,1)S(1)} fusion(bf16[1280,1728]{0,1:T(8,128)(2,1)} %param.18, s32[1024]{0:T(1024)S(1)} %pad_clamp_fusion), kind=kCustom, calls=%fused_computation | custom fusion | bytes 1967616 | tf_op jit(solution)/shard_map/jit(_take)/gather | solution.py:496
  202.4 6.6 %convolution_convert_fusion.2 = bf16[2048,384]{1,0:T(8,128)(2,1)} fusion(bf16[2048,1280]{1,0:T(8,128)(2,1)} %bitcast.9, bf16[384,1280]{1,0:T(8,128)(2,1)S(1)} %gather_fusion, pred[384]{0:T(512)(128)(4,1)S(1)} %compare_and_fusion), kind=kOutput, calls=%fused_computation.7 | convolution fusion | flops 2014543872 | bytes 7799168 | tf_op jit(solution)/shard_map/dot_general | solution.py:508
  209.0 0.0 all-reduce.2.cloned.1.call-update
  209.0 6.0 %gather_fusion.1 = bf16[384,1280]{1,0:T(8,128)(2,1)S(1)} fusion(bf16[1728,1280]{1,0:T(8,128)(2,1)} %param.19, s32[1024]{0:T(1024)S(1)} %pad_clamp_fusion), kind=kCustom, calls=%fused_computation.1 | custom fusion | bytes 1967616 | tf_op jit(solution)/shard_map/jit(_take)/gather | solution.py:497
  215.7 44.3 %all-reduce.2.cloned.1.call-done = bf16[2048,384]{1,0:T(8,128)(2,1)} async-done(((bf16[2048,384]{1,0:T(8,128)(2,1)}), bf16[2048,384]{1,0:T(8,128)(2,1)}) %all-reduce.2.cloned.1.call-update) | async-done | bytes 1572880 | tf_op jit(solution)/shard_map/psum | solution.py:466
  260.0 6.7 %convolution_convert_fusion = bf16[2048,1280]{1,0:T(8,128)(2,1)} fusion(bf16[2048,384]{1,0:T(8,128)(2,1)} %all-reduce.2.cloned.1.call-done, pred[384]{0:T(512)(128)(4,1)S(1)} %iota_compare_fusion, bf16[384,1280]{1,0:T(8,128)(2,1)S(1)} %gather_fusion.1, pred[384]{0:T(512)(128)(4,1)S(1)} %compare_and_fusion), kind=kOutput, calls=%fused_computation.2 | convolution fusion | flops 2019524608 | bytes 7799552 | tf_op jit(solution)/shard_map/dot_general | solution.py:515
  266.7 0.0 copy-start
  266.7 78.5 %shard_map.126 = f32[256,1280]{1,0:T(8,128)S(1)} custom-call(bf16[8,256,1280]{2,1,0:T(8,128)(2,1)} %bitcast.10), custom_call_target="tpu_custom_call" | custom-call | tf_op jit(solution)/shard_map/pallas_call | solution.py:445
  345.2 1.0 fusion.8
  346.2 0.0 copy-done
  346.2 0.5 fusion
  346.7 0.6 div.18
  (8 shorter events, 0.1 us)
Async XLA Ops:
  7.2 252.8 %all-reduce.2.cloned.1.call-start = ((), (), s32[]{:S(2)}) async-start(), calls=%async_computation | async-start | bytes 3145728 | tf_op jit(solution)/shard_map/psum | solution.py:466
  62.5 19.4 %copy-start.1 = (bf16[256,1280]{1,0:T(8,128)(2,1)S(1)}, bf16[256,1280]{1,0:T(8,128)(2,1)}, u32[]{:S(2)}) copy-start(bf16[256,1280]{1,0:T(8,128)(2,1)} %param.11) | copy-start | bytes 1966084
  62.5 25.4 %copy-start.3 = (bf16[1280]{0:T(1024)(128)(2,1)S(1)}, bf16[1280]{0:T(1024)(128)(2,1)}, u32[]{:S(2)}) copy-start(bf16[1280]{0:T(1024)(128)(2,1)} %param.17) | copy-start | bytes 7684
  89.0 107.2 %copy-start.2 = (s32[1,384]{1,0:T(1,128)S(1)}, s32[1,384]{1,0:T(1,128)}, u32[]{:S(2)}) copy-start(s32[1,384]{1,0:T(1,128)} %param.20) | copy-start | bytes 4612
  266.7 79.5 %copy-start = (bf16[2048,384]{1,0:T(8,128)(2,1)S(1)}, bf16[2048,384]{1,0:T(8,128)(2,1)}, u32[]{:S(2)}) copy-start(bf16[2048,384]{1,0:T(8,128)(2,1)} %all-reduce.2.cloned.1.call-done) | copy-start | bytes 4718596
Sparse Core Ops, SparseCore 0:
  209.2 50.7 all-reduce.1
